TPU v7x, 64 devices: a 2x2x8 block of a 4x4x8 slice. The times are simulated.
64 devices in a mesh: dp: 4 (over x, y), fsdp: 16 (over z, core).
Axes of the slice: x: 2, y: 2, z: 8, core: 2. Of those that a mesh axis runs over, the one named last changes fastest.
The devices are a block of a 4x4x8 slice.
Arguments:
- x: bfloat16 [64, 1024, 1152], P(('dp', 'fsdp')), parts along dimension 0
- w_q: bfloat16 [2, 1152, 1024], P(None, 'fsdp')
- w_k: bfloat16 [2, 1152, 256], P(None, 'fsdp')
- w_v: bfloat16 [2, 1152, 256], P(None, 'fsdp')
- w_o: bfloat16 [2, 1024, 1152], P(None, 'fsdp')
- w_gate: bfloat16 [2, 1152, 6912], P(None, 'fsdp')
- w_up: bfloat16 [2, 1152, 6912], P(None, 'fsdp')
- w_down: bfloat16 [2, 6912, 1152], P(None, 'fsdp')
- norm_w: float32 [2, 4, 1152], replicated
- qk_norm_w: float32 [2, 2, 256], replicated
Outputs:
- output 1: bfloat16 [64, 1024, 1152], P(('dp', 'fsdp')), parts along dimension 0
- output 2: bfloat16 [64, 1024, 1, 256], P(('dp', 'fsdp')), parts along dimension 0
- output 3: bfloat16 [64, 1024, 1, 256], P(('dp', 'fsdp')), parts along dimension 0
There are 4 independent parts. A program takes and returns all parts, laid end to end along the dimension named above; an argument that names none is the same for every part.
All inputs are finite; a program needn't handle non-finite values.
Results may differ from a plain program's by a relative error of at most 0.0142371.
Values are sent between devices in bfloat16 or wider.
A program may use at most 768 MiB of HBM per device.

v0:
```python
import jax
import jax.numpy as jnp
from jax import lax
from jax.sharding import PartitionSpec as P, NamedSharding

WINDOW = 1024
NORM_EPS = 1e-6
LOCAL_BASE = 10000.0
GLOBAL_BASE = 1000000.0
GLOBAL_POS_DIV = 8.0


def rms_norm(values, gain_w):
    mean_sq = jnp.mean(values * values, axis=-1, keepdims=True)
    return values * lax.rsqrt(mean_sq + NORM_EPS) * (1.0 + gain_w)


def rope_tables(seq_len, head_dim, rope_base, pos_div):
    half_dim = head_dim // 2
    inv_freq = rope_base ** (-2.0 * jnp.arange(half_dim, dtype=jnp.float32) / head_dim)
    positions = jnp.arange(seq_len, dtype=jnp.float32) / pos_div
    angles = positions[:, None] * inv_freq[None, :]
    return jnp.cos(angles), jnp.sin(angles)


def apply_rope(values, cos_t, sin_t):
    half_dim = values.shape[-1] // 2
    lo_half = values[..., :half_dim]
    hi_half = values[..., half_dim:]
    cos_b = cos_t[:, None, :]
    sin_b = sin_t[:, None, :]
    return jnp.concatenate([lo_half * cos_b - hi_half * sin_b, hi_half * cos_b + lo_half * sin_b], axis=-1)


def attend(query_bf, key_bf, value_bf, window, model_dim):
    num_seqs, seq_len, num_heads, head_dim = query_bf.shape
    kv_heads = key_bf.shape[2]
    groups = num_heads // kv_heads
    q_scalar = model_dim // num_heads if head_dim == 128 else head_dim
    q_scale = q_scalar ** -0.5
    q_block = min(seq_len, 512)
    num_blocks = seq_len // q_block
    key_span = min(seq_len, q_block + window)
    query_grp = query_bf.reshape(num_seqs, seq_len, kv_heads, groups, head_dim)

    def one_block(blk_idx):
        q_start = blk_idx * q_block
        k_start = jnp.maximum(q_start + q_block - key_span, 0)
        q_blk = lax.dynamic_slice_in_dim(query_grp, q_start, q_block, axis=1)
        k_blk = lax.dynamic_slice_in_dim(key_bf, k_start, key_span, axis=1)
        v_blk = lax.dynamic_slice_in_dim(value_bf, k_start, key_span, axis=1)
        scores = jnp.einsum('nqkgd,nskd->nkgqs', q_blk, k_blk, preferred_element_type=jnp.float32) * q_scale
        pos_diff = (q_start + jnp.arange(q_block))[:, None] - (k_start + jnp.arange(key_span))[None, :]
        allowed = (pos_diff >= 0) & (pos_diff < window)
        scores = jnp.where(allowed, scores, -1e30)
        probs_bf = jax.nn.softmax(scores, axis=-1).astype(jnp.bfloat16)
        block_out = jnp.einsum('nkgqs,nskd->nqkgd', probs_bf, v_blk, preferred_element_type=jnp.float32)
        return block_out.astype(jnp.bfloat16)

    block_outs = lax.map(one_block, jnp.arange(num_blocks))
    return jnp.moveaxis(block_outs, 0, 1).reshape(num_seqs, seq_len, num_heads * head_dim)


def decoder_layer(x, weights, norm_w, qk_norm_w, window, rope_base, pos_div):
    w_q, w_k, w_v, w_o, w_gate, w_up, w_down = weights
    num_seqs, seq_len, model_dim = x.shape
    head_dim = qk_norm_w.shape[-1]
    num_heads = w_q.shape[1] // head_dim
    kv_heads = w_k.shape[1] // head_dim
    x_f32 = x.astype(jnp.float32)
    normed = rms_norm(x_f32, norm_w[0]).astype(jnp.bfloat16)
    query_f32 = jnp.einsum('nsd,de->nse', normed, w_q, preferred_element_type=jnp.float32).reshape(num_seqs, seq_len, num_heads, head_dim)
    key_f32 = jnp.einsum('nsd,de->nse', normed, w_k, preferred_element_type=jnp.float32).reshape(num_seqs, seq_len, kv_heads, head_dim)
    value_bf = jnp.einsum('nsd,de->nse', normed, w_v, preferred_element_type=jnp.float32).astype(jnp.bfloat16).reshape(num_seqs, seq_len, kv_heads, head_dim)
    cos_t, sin_t = rope_tables(seq_len, head_dim, rope_base, pos_div)
    query_bf = apply_rope(rms_norm(query_f32, qk_norm_w[0]), cos_t, sin_t).astype(jnp.bfloat16)
    key_bf = apply_rope(rms_norm(key_f32, qk_norm_w[1]), cos_t, sin_t).astype(jnp.bfloat16)
    attn_out = attend(query_bf, key_bf, value_bf, window, model_dim)
    attn_proj = jnp.einsum('nse,ed->nsd', attn_out, w_o, preferred_element_type=jnp.float32)
    resid = (x_f32 + rms_norm(attn_proj, norm_w[1])).astype(jnp.bfloat16)
    resid_f32 = resid.astype(jnp.float32)
    normed_ffn = rms_norm(resid_f32, norm_w[2]).astype(jnp.bfloat16)
    gate_f32 = jnp.einsum('nsd,df->nsf', normed_ffn, w_gate, preferred_element_type=jnp.float32)
    up_f32 = jnp.einsum('nsd,df->nsf', normed_ffn, w_up, preferred_element_type=jnp.float32)
    hidden_act = (jax.nn.gelu(gate_f32, approximate=True) * up_f32).astype(jnp.bfloat16)
    down_f32 = jnp.einsum('nsf,fd->nsd', hidden_act, w_down, preferred_element_type=jnp.float32)
    layer_out = (resid_f32 + rms_norm(down_f32, norm_w[3])).astype(jnp.bfloat16)
    return layer_out, key_bf, value_bf


def gather_layer(stacked, layer_idx):
    return tuple(lax.all_gather(w_all[layer_idx], 'fsdp', axis=0, tiled=True) for w_all in stacked)


def solution(mesh):
    batch_spec = P(('dp', 'fsdp'), None, None)
    cache_spec = P(('dp', 'fsdp'), None, None, None)
    weight_spec = P(None, 'fsdp', None)
    rep_spec = P()

    def per_device(x, w_q, w_k, w_v, w_o, w_gate, w_up, w_down, norm_w, qk_norm_w):
        stacked = (w_q, w_k, w_v, w_o, w_gate, w_up, w_down)
        local_w = gather_layer(stacked, 0)
        hidden = decoder_layer(x, local_w, norm_w[0], qk_norm_w[0], WINDOW, LOCAL_BASE, 1.0)[0]
        global_w = gather_layer(stacked, 1)
        return decoder_layer(hidden, global_w, norm_w[1], qk_norm_w[1], x.shape[1], GLOBAL_BASE, GLOBAL_POS_DIV)

    in_specs = (batch_spec,) + (weight_spec,) * 7 + (rep_spec, rep_spec)
    return jax.shard_map(per_device, mesh=mesh, in_specs=in_specs, out_specs=(batch_spec, cache_spec, cache_spec), check_vma=False)
```

profile of v0, /device:TPU:22, one launch (start us, length us, event | category | flops | bytes accessed | tf_op | source)
XLA Modules:
  0.0 724.6 jit_solution(17151072804448160326)
XLA Ops:
  11.1 2.9 fusion.158
  15.7 3.1 fusion.159
  27.1 24.2 %all-gather.1 = bf16[1,1152,256]{2,1,0:T(8,128)(2,1)S(1)} all-gather(bf16[1,72,256]{2,1,0:T(8,128)(2,1)S(1)} %get-tuple-element.342), channel_id=3, replica_groups=mesh['dp'=4,'fsdp'=16] {'fsdp'}, dimensions={1}, use_global_device_ids=true | all-gather | bytes 626688 | tf_op jit(solution)/shard_map/all_gather | solution.py:92
  52.6 2.3 subtract_convert_fusion.2
  57.8 18.0 %all-gather.2 = bf16[1,1152,256]{2,1,0:T(8,128)(2,1)S(1)} all-gather(bf16[1,72,256]{2,1,0:T(8,128)(2,1)S(1)} %get-tuple-element.340), channel_id=4, replica_groups=mesh['dp'=4,'fsdp'=16] {'fsdp'}, dimensions={1}, use_global_device_ids=true | all-gather | bytes 626688 | tf_op jit(solution)/shard_map/all_gather | solution.py:92
  77.5 18.2 %all-gather.9 = bf16[1,1152,256]{2,1,0:T(8,128)(2,1)} all-gather(bf16[1,72,256]{2,1,0:T(8,128)(2,1)S(1)} %get-tuple-element.339), channel_id=11, replica_groups=mesh['dp'=4,'fsdp'=16] {'fsdp'}, dimensions={1}, use_global_device_ids=true | all-gather | bytes 626688 | tf_op jit(solution)/shard_map/all_gather | solution.py:92
  95.7 19.7 %all-gather.8 = bf16[1,1152,256]{2,1,0:T(8,128)(2,1)} all-gather(bf16[1,72,256]{2,1,0:T(8,128)(2,1)S(1)} %get-tuple-element.341), channel_id=10, replica_groups=mesh['dp'=4,'fsdp'=16] {'fsdp'}, dimensions={1}, use_global_device_ids=true | all-gather | bytes 626688 | tf_op jit(solution)/shard_map/all_gather | solution.py:92
  115.4 3.1 multiply_cosine_fusion.1
  118.5 6.6 fusion.106
  125.1 5.4 copy.18
  130.5 2.9 multiply_reduce_fusion.5
  138.7 23.4 %while.28 = (s32[]{:T(128)}, bf16[2,1,512,1,4,256]{5,4,2,0,3,1:T(4,128)(2,1)}, s32[2]{0:T(128)S(1)}, bf16[1,1024,1,4,256]{4,1,3,2,0:T(8,128)(2,1)}, bf16[1,1024,...) while((s32[]{:T(128)}, ...), condition=%wide.region_6.7_spmd, body=%wide.region_3.6_spmd.sunk | while | flops 2175268352 | bytes 32559820 | solution.py:60
  140.5 3.0 fusion.199
  143.5 2.3 fusion.200
  145.8 2.7 fusion.201
  152.1 3.0 fusion.199
  155.1 2.3 fusion.200
  157.4 2.7 fusion.201
  162.1 3.4 copy.29
  165.5 5.2 multiply_reduce_fusion.3
  170.8 2.6 fusion.84
  173.4 5.4 all-gather.29.cloned.1.call-done
  178.7 27.6 %fusion.70 = f32[1024,6912]{1,0:T(8,128)} fusion(bf16[1,1152,6912]{2,1,0:T(8,128)(2,1)} %all-gather.29.cloned.1.call-done, bf16[1,1024,1152]{2,1,0:T(8,128)(2,1)} %get-tuple-element.316, f32[1152]{0:T(1024)S(1)} %get-tuple-element.283, f32[1024]{0:T(1024)S(1)} %add_rsqrt_fusion.8), kind=kOutput, calls=%fused_computation.76 | convolution fusion | flops 16312172544 | bytes 46604800 | tf_op jit(solution)/shard_map/nsd,df->nsf/dot_general | solution.py:83
  206.3 60.4 %all-gather.31.cloned.1.call-done = bf16[1,1152,6912]{2,1,0:T(8,128)(2,1)} async-done(((bf16[1,72,6912]{2,1,0:T(8,128)(2,1)}), bf16[1,1152,6912]{2,1,0:T(8,128)(2,1)}) %all-gather.31.cloned.1.call-update) | async-done | bytes 15925264 | tf_op jit(solution)/shard_map/all_gather | solution.py:92
  266.7 29.6 %fusion.48.clone.1.clone.2 = bf16[1024,6912]{1,0:T(8,128)(2,1)} fusion(f32[1024,6912]{1,0:T(8,128)} %fusion.70, bf16[1,1152,6912]{2,1,0:T(8,128)(2,1)} %all-gather.31.cloned.1.call-done, bf16[1,1024,1152]{2,1,0:T(8,128)(2,1)S(1)} %copy-done.5, f32[1152]{0:T(1024)S(1)} %get-tuple-element.283, f32[1024]{0:T(1024)S(1)} %add_rsqrt_fusion.8), kind=kOutput, calls=%fused_computation.58.clone.clone.clone.clone.clone | convolution fusion | flops 16382951424 | bytes 60760576 | tf_op jit(solution)/shard_map/nsd,df->nsf/dot_general | solution.py:84
  296.3 58.5 %all-gather.33.cloned.1.call-done = bf16[1,6912,1152]{2,1,0:T(8,128)(2,1)} async-done(((bf16[1,432,1152]{2,1,0:T(8,128)(2,1)}), bf16[1,6912,1152]{2,1,0:T(8,128)(2,1)}) %all-gather.33.cloned.1.call-update) | async-done | bytes 15925264 | tf_op jit(solution)/shard_map/all_gather | solution.py:92
  354.8 23.3 %multiply_reduce_fusion.2 = (f32[1024]{0:T(1024)S(1)}, f32[1024,1152]{1,0:T(8,128)S(1)}) fusion(bf16[1,6912,1152]{2,1,0:T(8,128)(2,1)} %all-gather.33.cloned.1.call-done, bf16[1024,6912]{1,0:T(8,128)(2,1)} %fusion.48.clone.1.clone.2), kind=kOutput, calls=%fused_computation.116 | convolution fusion | flops 16309812224 | bytes 34803712 | tf_op jit(solution)/shard_map/nsf,fd->nsd/dot_general | solution.py:86
  380.8 2.5 fusion.131
  383.5 8.0 %all-gather.35.cloned.1.call-done = bf16[1,1152,1024]{2,1,0:T(8,128)(2,1)} async-done(((bf16[1,72,1024]{2,1,0:T(8,128)(2,1)}), bf16[1,1152,1024]{2,1,0:T(8,128)(2,1)}) %all-gather.35.cloned.1.call-update) | async-done | bytes 2359312 | tf_op jit(solution)/shard_map/all_gather | solution.py:92
  391.5 6.6 fusion.102
  398.1 5.4 copy.21
  403.5 2.9 multiply_reduce_fusion.4
  412.6 23.4 %while.29 = (s32[]{:T(128)}, bf16[2,1,512,1,4,256]{5,4,2,0,3,1:T(4,128)(2,1)}, s32[2]{0:T(128)S(1)}, bf16[1,1024,1,4,256]{4,1,3,2,0:T(8,128)(2,1)}, bf16[1,1024,...) while((s32[]{:T(128)}, ...), condition=%wide.region_16.17_spmd, body=%wide.region_13.16_spmd.sunk | while | flops 2175268352 | bytes 32559820 | solution.py:60
  414.4 3.0 fusion.205
  417.4 2.3 fusion.206
  419.7 2.7 fusion.207
  426.0 3.0 fusion.205
  429.0 2.3 fusion.206
  431.3 2.7 fusion.207
  436.1 2.5 copy.30
  438.6 4.8 multiply_reduce_fusion.1
  444.6 71.0 %all-gather.39.cloned.1.call-done = bf16[1,1152,6912]{2,1,0:T(8,128)(2,1)} async-done(((bf16[1,72,6912]{2,1,0:T(8,128)(2,1)}), bf16[1,1152,6912]{2,1,0:T(8,128)(2,1)}) %all-gather.39.cloned.1.call-update) | async-done | bytes 15925264 | tf_op jit(solution)/shard_map/all_gather | solution.py:92
  515.6 25.5 %fusion.63 = f32[1024,6912]{1,0:T(8,128)} fusion(bf16[1,1152,6912]{2,1,0:T(8,128)(2,1)} %all-gather.39.cloned.1.call-done, bf16[1,1024,1152]{2,1,0:T(8,128)(2,1)S(1)} %get-tuple-element.312, f32[1152]{0:T(1024)S(1)} %copy-done.22, f32[1024]{0:T(1024)S(1)} %add_rsqrt_fusion.3), kind=kOutput, calls=%fused_computation.71 | convolution fusion | flops 16312172544 | bytes 46604800 | tf_op jit(solution)/shard_map/nsd,df->nsf/dot_general | solution.py:83
  541.1 62.7 %all-gather.41.cloned.1.call-done = bf16[1,1152,6912]{2,1,0:T(8,128)(2,1)} async-done(((bf16[1,72,6912]{2,1,0:T(8,128)(2,1)}), bf16[1,1152,6912]{2,1,0:T(8,128)(2,1)}) %all-gather.41.cloned.1.call-update) | async-done | bytes 15925264 | tf_op jit(solution)/shard_map/all_gather | solution.py:92
  603.8 29.3 %fusion.57.clone.1.clone.4 = bf16[1024,6912]{1,0:T(8,128)(2,1)} fusion(f32[1024,6912]{1,0:T(8,128)} %fusion.63, bf16[1,1152,6912]{2,1,0:T(8,128)(2,1)} %all-gather.41.cloned.1.call-done, bf16[1,1024,1152]{2,1,0:T(8,128)(2,1)S(1)} %get-tuple-element.312, f32[1152]{0:T(1024)S(1)} %copy-done.22, f32[1024]{0:T(1024)S(1)} %add_rsqrt_fusion.3), kind=kOutput, calls=%fused_computation.67.clone.clone.clone.clone.clone.1 | convolution fusion | flops 16382951424 | bytes 60760576 | tf_op jit(solution)/shard_map/nsd,df->nsf/dot_general | solution.py:84
  633.2 58.7 %all-gather.43.cloned.1.call-done = bf16[1,6912,1152]{2,1,0:T(8,128)(2,1)} async-done(((bf16[1,432,1152]{2,1,0:T(8,128)(2,1)}), bf16[1,6912,1152]{2,1,0:T(8,128)(2,1)}) %all-gather.43.cloned.1.call-update) | async-done | bytes 15925264 | tf_op jit(solution)/shard_map/all_gather | solution.py:92
  691.9 23.2 %multiply_reduce_fusion = (f32[1024]{0:T(1024)S(1)}, f32[1024,1152]{1,0:T(8,128)S(1)}) fusion(bf16[1,6912,1152]{2,1,0:T(8,128)(2,1)} %all-gather.43.cloned.1.call-done, bf16[1024,6912]{1,0:T(8,128)(2,1)} %fusion.57.clone.1.clone.4), kind=kOutput, calls=%fused_computation.114 | convolution fusion | flops 16309812224 | bytes 34803712 | tf_op jit(solution)/shard_map/nsf,fd->nsd/dot_general | solution.py:86
  715.1 2.2 fusion.95
  (155 shorter events, 46.6 us)
Async XLA Ops:
  7.2 7.0 copy-start.9
  7.2 111.3 %all-gather.25.cloned.1.call-start = ((), (), s32[]{:S(2)}) async-start(), calls=%async_computation | async-start | bytes 2506752 | tf_op jit(solution)/shard_map/all_gather | solution.py:92
  9.1 156.4 %all-gather.27.cloned.1.call-start = ((), (), s32[]{:S(2)}) async-start(), calls=%async_computation.1 | async-start | bytes 2506752 | tf_op jit(solution)/shard_map/all_gather | solution.py:92
  11.0 167.7 %all-gather.29.cloned.1.call-start = ((), (), s32[]{:S(2)}) async-start(), calls=%async_computation.2 | async-start | bytes 16920576 | tf_op jit(solution)/shard_map/all_gather | solution.py:92
  14.1 252.7 %all-gather.31.cloned.1.call-start = ((), (), s32[]{:S(2)}) async-start(), calls=%async_computation.3 | async-start | bytes 16920576 | tf_op jit(solution)/shard_map/all_gather | solution.py:92
  15.6 7.7 %copy-start.18 = (f32[2,4,1152]{2,1,0:T(4,128)S(1)}, f32[2,4,1152]{2,1,0:T(4,128)}, u32[]{:S(2)}) copy-start(f32[2,4,1152]{2,1,0:T(4,128)} %param.22) | copy-start | bytes 110596
  15.6 8.4 %copy-start.2 = (bf16[1,1024,1152]{2,1,0:T(8,128)(2,1)S(1)}, bf16[1,1024,1152]{2,1,0:T(8,128)(2,1)}, u32[]{:S(2)}) copy-start(bf16[1,1024,1152]{2,1,0:T(8,128)(2,1)} %param.14) | copy-start | bytes 7077892
  15.6 8.9 %copy-start.26 = (f32[2,2,256]{2,1,0:T(2,128)S(1)}, f32[2,2,256]{2,1,0:T(2,128)}, u32[]{:S(2)}) copy-start(f32[2,2,256]{2,1,0:T(2,128)} %param.23) | copy-start | bytes 12292
  15.7 339.1 %all-gather.33.cloned.1.call-start = ((), (), s32[]{:S(2)}) async-start(), calls=%async_computation.4 | async-start | bytes 16920576 | tf_op jit(solution)/shard_map/all_gather | solution.py:92
  18.9 8.2 %copy-start.14 = (bf16[2,72,256]{2,1,0:T(8,128)(2,1)S(1)}, bf16[2,72,256]{2,1,0:T(8,128)(2,1)}, u32[]{:S(2)}) copy-start(bf16[2,72,256]{2,1,0:T(8,128)(2,1)} %param.16) | copy-start | bytes 221188
  18.9 372.6 %all-gather.35.cloned.1.call-start = ((), (), s32[]{:S(2)}) async-start(), calls=%async_computation.5 | async-start | bytes 2506752 | tf_op jit(solution)/shard_map/all_gather | solution.py:92
  19.6 419.0 %all-gather.37.cloned.1.call-start = ((), (), s32[]{:S(2)}) async-start(), calls=%async_computation.6 | async-start | bytes 2506752 | tf_op jit(solution)/shard_map/all_gather | solution.py:92
  20.4 495.3 %all-gather.39.cloned.1.call-start = ((), (), s32[]{:S(2)}) async-start(), calls=%async_computation.7 | async-start | bytes 16920576 | tf_op jit(solution)/shard_map/all_gather | solution.py:92
  21.2 582.6 %all-gather.41.cloned.1.call-start = ((), (), s32[]{:S(2)}) async-start(), calls=%async_computation.8 | async-start | bytes 16920576 | tf_op jit(solution)/shard_map/all_gather | solution.py:92
  22.0 669.9 %all-gather.43.cloned.1.call-start = ((), (), s32[]{:S(2)}) async-start(), calls=%async_computation.9 | async-start | bytes 16920576 | tf_op jit(solution)/shard_map/all_gather | solution.py:92
  22.6 2.5 copy-start.29
  22.7 92.7 %copy-start.16 = (f32[1024]{0:T(1024)}, f32[1024]{0:T(1024)S(1)}, u32[]{:S(2)}) copy-start(f32[1024]{0:T(1024)S(1)} %iota_multiply_fusion.2) | copy-start | bytes 12292
  27.1 25.5 %copy-start.30 = (f32[128]{0:T(128)S(1)}, f32[128]{0:T(128)}, u32[]{:S(2)}) copy-start(f32[128]{0:T(128)} %copy-done.29) | copy-start | bytes 1540
  51.3 6.5 copy-start.15
  75.8 39.6 %copy-start.27 = (f32[128]{0:T(128)S(1)}, f32[128]{0:T(128)}, u32[]{:S(2)}) copy-start(f32[128]{0:T(128)} %fusion.138) | copy-start | bytes 1540
  130.5 3.4 copy-start.1
  135.2 3.5 copy-start.13
  135.2 3.5 copy-start.32
  178.7 88.0 %copy-start.5 = (bf16[1,1024,1152]{2,1,0:T(8,128)(2,1)S(1)}, bf16[1,1024,1152]{2,1,0:T(8,128)(2,1)}, u32[]{:S(2)}) copy-start(bf16[1,1024,1152]{2,1,0:T(8,128)(2,1)} %get-tuple-element.316) | copy-start | bytes 7077892
  296.3 81.8 %copy-start.21 = (f32[1152]{0:T(1024)S(1)}, f32[1152]{0:T(1024)}, u32[]{:S(2)}) copy-start(f32[1152]{0:T(1024)} %get-tuple-element.282) | copy-start | bytes 13828
  354.8 23.4 %copy-start.6 = (bf16[1,1024,1152]{2,1,0:T(8,128)(2,1)S(1)}, bf16[1,1024,1152]{2,1,0:T(8,128)(2,1)}, u32[]{:S(2)}) copy-start(bf16[1,1024,1152]{2,1,0:T(8,128)(2,1)} %get-tuple-element.316) | copy-start | bytes 7077892
  378.2 1.3 copy-start.11
  378.2 1.3 copy-start.23
  379.4 30.4 %copy-start.3 = (bf16[1,1024,1152]{2,1,0:T(8,128)(2,1)}, bf16[1,1024,1152]{2,1,0:T(8,128)(2,1)S(1)}, u32[]{:S(2)}) copy-start(bf16[1,1024,1152]{2,1,0:T(8,128)(2,1)S(1)} %get-tuple-element.314) | copy-start | bytes 7077892
  379.4 1.2 copy-start.25
  379.4 1.4 copy-start.17
  379.4 1.4 copy-start.28
  398.1 8.3 %copy-start.24 = (f32[1,1,256]{2,1,0:T(1,128)S(1)}, f32[1,1,256]{2,1,0:T(1,128)}, u32[]{:S(2)}) copy-start(f32[1,1,256]{2,1,0:T(1,128)} %get-tuple-element.348) | copy-start | bytes 3076
  403.5 3.4 copy-start
  406.4 1.3 copy-start.7
  406.4 1.3 copy-start.8
  407.7 2.1 copy-start.10
  436.0 7.3 %copy-start.12 = (bf16[1,1024,1,256]{3,1,2,0:T(8,128)(2,1)}, bf16[1,1024,1,256]{3,1,2,0:T(8,128)(2,1)S(1)}, u32[]{:S(2)}) copy-start(bf16[1,1024,1,256]{3,1,2,0:T(8,128)(2,1)S(1)} %get-tuple-element.541) | copy-start | bytes 1572868
  436.0 7.3 %copy-start.31 = (bf16[1,1024,1,256]{3,1,2,0:T(8,128)(2,1)}, bf16[1,1024,1,256]{3,1,2,0:T(8,128)(2,1)S(1)}, u32[]{:S(2)}) copy-start(bf16[1,1024,1,256]{3,1,2,0:T(8,128)(2,1)S(1)} %get-tuple-element.552) | copy-start | bytes 1572868
  438.6 4.8 copy-start.4
  438.6 4.8 copy-start.20
  443.4 72.2 %copy-start.22 = (f32[1152]{0:T(1024)S(1)}, f32[1152]{0:T(1024)}, u32[]{:S(2)}) copy-start(f32[1152]{0:T(1024)} %get-tuple-element.286) | copy-start | bytes 13828
  633.2 81.9 %copy-start.19 = (f32[1152]{0:T(1024)S(1)}, f32[1152]{0:T(1024)}, u32[]{:S(2)}) copy-start(f32[1152]{0:T(1024)} %get-tuple-element.279) | copy-start | bytes 13828
Sparse Core Ops, SparseCore 0:
  10.2 40.4 all-gather.24
  52.3 35.4 all-gather.26
  89.5 89.2 all-gather.28
  180.2 86.4 all-gather.30
  268.2 86.5 all-gather.32
  356.3 35.1 all-gather.34
  393.1 34.7 all-gather.36
  429.5 86.0 all-gather.38
  517.3 86.5 all-gather.40
  605.3 86.5 all-gather.42
where the time goes:
time: 733 us; the launch traced here: 725 us
  waiting for transfers between devices  328 us (45%)
  matrix products  209 us (29%)
  blocking collectives  80.1 us (11%)
  local copies, waits for them, and re-layouts  44.5 us (6%)
  other arithmetic  43.6 us (6%)
  between operations  15.2 us (2%)
    all_gather x10, waiting for transfers between devices, gather_layer(): lax.all_gather(w_all[layer_idx], 'fsdp', axis=0, tiled=True)  325 us
    all_gather x4, blocking collectives, gather_layer(): lax.all_gather(w_all[layer_idx], 'fsdp', axis=0, tiled=True)  80.1 us
    dot_general x2, matrix products, decoder_layer(): jnp.einsum('nsd,df->nsf', normed_ffn, w_up, preferred_element_type=jnp.fl...  58.9 us
    dot_general x2, matrix products, decoder_layer(): jnp.einsum('nsd,df->nsf', normed_ffn, w_gate, preferred_element_type=jnp....  53.1 us
    dot_general x2, matrix products, decoder_layer(): jnp.einsum('nsf,fd->nsd', hidden_act, w_down, preferred_element_type=jnp....  46.5 us
  transfers between devices with their start and end apart: 10, of which 7 were waited for; matrix products, arithmetic and copies ran while one was open for 37% of the time, Pallas kernels for 0%

commit v1 on v0

v1 whole, which is shorter than its diff:
```python
import functools
import math

import jax
import jax.numpy as jnp
from jax import lax
from jax.experimental import pallas as pl
from jax.experimental.pallas import tpu as pltpu
from jax.sharding import PartitionSpec as P

WINDOW = 1024
NORM_EPS = 1e-6
ROPE_BASES = (10000.0, 1000000.0)
ROPE_DIVS = (1.0, 8.0)
MESH = pl.DeviceIdType.MESH
LANES = 128
DELTA = 2
SLOTS = 8
PIECES = 4


class Comm:
    def __init__(self, side, nz, ng, s_ref, g_ref, ssem, rsem, lsem):
        self.ng, self.nz, self.s, self.g = ng, nz, s_ref, g_ref
        self.ssem, self.rsem, self.lsem = ssem, rsem, lsem
        d, f = lax.axis_index("dp"), lax.axis_index("fsdp")
        self.z, self.c = f // 2, f % 2
        xi, yi = d // side, d % side
        a, b = xi % 2, yi % 2
        self.h = (a + b) % 2
        self.up = {"dp": d, "fsdp": ((self.z + 1) % nz) * 2 + self.c}
        self.down = {"dp": d, "fsdp": ((self.z + nz - 1) % nz) * 2 + self.c}
        self.sib = {"dp": d, "fsdp": self.z * 2 + 1 - self.c}
        self.over_x = {"dp": (xi + 1 - 2 * a) * side + yi, "fsdp": f}
        self.over_y = {"dp": xi * side + yi + 1 - 2 * b, "fsdp": f}
        self.hops = nz // 2
        self.stages = self.hops + 2

    def barrier(self):
        bar = pltpu.get_barrier_semaphore()
        peers = (self.up, self.down, self.sib, self.over_x, self.over_y)
        for peer in peers:
            pl.semaphore_signal(bar, inc=1, device_id=peer, device_id_type=MESH)
        pl.semaphore_wait(bar, len(peers))

    def copies(self, k, g, slot):
        rows, nz, n = self.s.shape[2], self.nz, 2 * self.hops
        mine = pl.ds(pl.multiple_of(self.c * rows, 8), rows)

        def remote(i, src, dst, peer):
            return pltpu.make_async_remote_copy(
                src_ref=src, dst_ref=dst, send_sem=self.ssem.at[i, slot], recv_sem=self.rsem.at[i, slot],
                device_id=peer, device_id_type=MESH)

        if k < self.hops:
            half = k == self.hops - 1
            pu = pl.ds(2 * self.h, 1 if half else 2)
            pd = pl.ds(2 * self.h + 1, 1) if half else pu
            if k == 0:
                su, sd = self.s.at[g, pu], self.s.at[g, pd]
            else:
                su, sd = self.g.at[g, pu, nz - k, mine], self.g.at[g, pd, k, mine]
            out = [remote(2 * k, su, self.g.at[g, pu, nz - 1 - k, mine], self.up),
                   remote(2 * k + 1, sd, self.g.at[g, pd, k + 1, mine], self.down)]
            if k == 0:
                out.append(remote(n + 3, self.s.at[g], self.g.at[g, :, 0, mine], self.sib))
            return out
        rest = pl.ds(1, nz - 1)
        if k == self.hops:
            p = 2 * self.h
            px, py = self.g.at[g, p, rest, mine], self.g.at[g, p + 1, rest, mine]
            return [remote(n, px, px, self.over_x), remote(n + 1, py, py, self.over_y)]
        both = self.g.at[g, :, rest, mine]
        return [remote(n + 2, both, both, self.sib)]

    def own(self, g, slot):
        rows = self.s.shape[2]
        mine = pl.ds(pl.multiple_of(self.c * rows, 8), rows)
        return pltpu.make_async_copy(self.s.at[g], self.g.at[g, :, 0, mine], self.lsem.at[slot])

    def tick(self, t):
        slot, old = t % SLOTS, (t + SLOTS - DELTA) % SLOTS

        @pl.when(t < self.ng)
        def _():
            for cp in self.copies(0, t, slot):
                cp.start()
            self.own(t, slot).start()

        for k in range(1, self.stages + 1):
            g = t - DELTA * k

            @pl.when((g >= 0) & (g < self.ng))
            def _(k=k, g=g):
                for cp in self.copies(k - 1, g, old):
                    cp.wait()
                if k == 1:
                    self.own(g, old).wait()
                if k < self.stages:
                    for cp in self.copies(k, g, slot):
                        cp.start()

    def ticks(self, first, count):
        def body(i, carry):
            self.tick(first + i)
            return carry
        lax.fori_loop(0, count, body, 0)


def rms(values, gain):
    mean_sq = jnp.mean(values * values, axis=-1, keepdims=True)
    return values * lax.rsqrt(mean_sq + NORM_EPS) * (1.0 + gain)


def rope(values, cos_t, sin_t):
    half = values.shape[-1] // 2
    lo, hi = values[:, :half], values[:, half:]
    return jnp.concatenate([lo * cos_t - hi * sin_t, hi * cos_t + lo * sin_t], axis=-1)


def dot(a, b):
    return jnp.dot(a, b, preferred_element_type=jnp.float32)


def kernel(cfg, x_hbm, nw, qkn, tab, s_hbm, xo_hbm, ko_hbm, vo_hbm, g_hbm,
           xs, hs, x1, qs, ks, vs, at, ob, us, ys, wb, db,
           ssem, rsem, lsem, wsem, osem, dsem, iosem):
    side, nz, ng, layers, heads, hd, nf, nd, scale = cfg
    seq, dm = xs.shape
    rows_o = ob.shape[1] // (2 * nz)
    rows_d = db.shape[2] // (2 * nz)
    rows = s_hbm.shape[2]
    nsub = rows_d // rows
    ncol = dm // LANES
    per = ng // layers
    cm = Comm(side, nz, ng, s_hbm, g_hbm, ssem, rsem, lsem)
    cm.barrier()
    load_x = pltpu.make_async_copy(x_hbm, xs, iosem.at[0])
    load_x.start()
    lead = DELTA * cm.stages + 1
    first = lead + 2
    g_qkv, g_o, g_f, g_d = 0, 3, 6, 6 + nf
    MB = 256

    def place(rel):
        return (cm.z + rel) % nz

    def load_w(g, slot):
        for rel in range(nz):
            dst = wb.at[slot, :, pl.ds(pl.multiple_of(place(rel) * 2 * rows, 16), 2 * rows), :]
            pltpu.make_async_copy(g_hbm.at[g, :, rel], dst, wsem.at[slot]).start()

    def wait_w(slot):
        pltpu.make_async_copy(wb.at[slot], wb.at[slot], wsem.at[slot]).wait()

    def load_o(base):
        for i in range(pl.cdiv(ncol, PIECES)):
            n = min(PIECES, ncol - PIECES * i)
            for rel in range(nz):
                for c in range(2):
                    src = g_hbm.at[base + g_o + i, pl.ds(0, n), rel, pl.ds(c * rows, rows_o), :]
                    off = pl.multiple_of((place(rel) * 2 + c) * rows_o, 16)
                    dst = ob.at[pl.ds(PIECES * i, n), pl.ds(off, rows_o), :]
                    pltpu.make_async_copy(src, dst, osem.at[0]).start()

    def wait_o():
        pltpu.make_async_copy(ob, ob, osem.at[0]).wait()

    def load_d(base, batch, slot):
        for r in range(nsub):
            for rel in range(nz):
                for c in range(2):
                    src = g_hbm.at[base + g_d + batch * nsub + r, :, rel, pl.ds(c * rows, rows), :]
                    off = pl.multiple_of((place(rel) * 2 + c) * rows_d + r * rows, 8)
                    dst = db.at[slot, :, pl.ds(off, rows), :]
                    pltpu.make_async_copy(src, dst, dsem.at[slot]).start()

    def wait_d(slot):
        pltpu.make_async_copy(db.at[slot], db.at[slot], dsem.at[slot]).wait()

    def load_tail(base, slot):
        for r in range(nsub):
            for rel in range(nz):
                for c in range(2):
                    g = base + g_d + (ncol // PIECES) * nsub + r // PIECES
                    src = g_hbm.at[g, r % PIECES, rel, pl.ds(c * rows, rows), :]
                    off = pl.multiple_of((place(rel) * 2 + c) * rows_d + r * rows, 8)
                    dst = db.at[slot, 0, pl.ds(off, rows), :]
                    pltpu.make_async_copy(src, dst, dsem.at[slot]).start()

    def wait_tail(slot):
        pltpu.make_async_copy(db.at[slot, 0], db.at[slot, 0], dsem.at[slot]).wait()

    def blocks(n, size, body):
        def step(i, carry):
            body(i, pl.ds(pl.multiple_of(i * size, size), size))
            return carry
        lax.fori_loop(0, n // size, step, 0)

    cm.ticks(0, 1)
    load_x.wait()

    def norm_in(i, r):
        hs[r, :] = rms(xs[r, :].astype(jnp.float32), nw[0, pl.ds(0, 1), :]).astype(jnp.bfloat16)
    blocks(seq, MB, norm_in)
    cm.ticks(1, first - 1)

    def pair(ref, p):
        return jnp.concatenate([ref[2 * p], ref[2 * p + 1]], axis=-1)

    def layer(l, carry):
        base = l * per
        t0 = base + first

        load_w(base, 0)

        def head_out(r, acc, which):
            out = rms(acc, qkn[l, pl.ds(which, 1), :])
            return rope(out, tab[l, 0, r, :], tab[l, 1, r, :]).astype(jnp.bfloat16)

        for i in range(2):
            load_w(base + i + 1, (i + 1) % 2)
            wait_w(i % 2)

            def q_block(j, r, i=i):
                for p in range(2):
                    qs[2 * i + p, r, :] = head_out(r, dot(hs[r, :], pair(wb.at[i % 2], p)), 0)
            blocks(seq, MB, q_block)
            cm.tick(t0 + i)
        wait_w(0)

        def kv_block(j, r):
            ks[r, :] = head_out(r, dot(hs[r, :], pair(wb.at[0], 0)), 1)
            vs[r, :] = dot(hs[r, :], pair(wb.at[0], 1)).astype(jnp.bfloat16)
        blocks(seq, MB, kv_block)
        cm.tick(t0 + 2)
        load_o(base)
        done = 3

        @pl.when(l == layers - 1)
        def _():
            pltpu.make_async_copy(ks, ko_hbm, iosem.at[1]).start()
            pltpu.make_async_copy(vs, vo_hbm, iosem.at[2]).start()

        nb = seq // MB
        for b in range(nb):
            r = pl.ds(b * MB, MB)
            span = (b + 1) * MB
            per_tick = heads if b < nb // 2 else heads // 2

            def one_head(j, b=b, r=r, span=span):
                sc = lax.dot_general(qs[j, r, :], ks[pl.ds(0, span), :], (((1,), (1,)), ((), ())),
                                     preferred_element_type=jnp.float32) * scale
                diff = (b * MB + lax.broadcasted_iota(jnp.int32, sc.shape, 0)
                        - lax.broadcasted_iota(jnp.int32, sc.shape, 1))
                allowed = diff >= 0
                if span > WINDOW:
                    allowed = allowed & ((diff < WINDOW) | (l > 0))
                sc = jnp.where(allowed, sc, -1e30)
                e = jnp.exp(sc - jnp.max(sc, axis=-1, keepdims=True))
                probs = (e * (1.0 / jnp.sum(e, axis=-1, keepdims=True))).astype(jnp.bfloat16)
                at[j, r, :] = dot(probs, vs[pl.ds(0, span), :]).astype(jnp.bfloat16)

            for first_head in range(0, heads, per_tick):
                def body(j, carry):
                    one_head(j)
                    return carry
                lax.fori_loop(first_head, first_head + per_tick, body, 0)
                cm.tick(t0 + done)
                done += 1

        load_w(base + g_f, 0)
        wait_o()

        def o_block(i, r):
            lhs = jnp.concatenate([at[j, r, :] for j in range(heads)], axis=-1)
            parts = [dot(lhs, pair(ob, p)) for p in range(ncol // 2)]
            if ncol % 2:
                parts.append(dot(lhs, ob[ncol - 1]))
            proj = jnp.concatenate(parts, axis=-1)
            res = (xs[r, :].astype(jnp.float32) + rms(proj, nw[l, pl.ds(1, 1), :])).astype(jnp.bfloat16)
            x1[r, :] = res
            hs[r, :] = rms(res.astype(jnp.float32), nw[l, pl.ds(2, 1), :]).astype(jnp.bfloat16)
        blocks(seq, MB, o_block)
        cm.ticks(t0 + done, 2)
        done += 2

        def gu(j, slot, last=False):
            if not last:
                load_w(base + g_f + j + 1, 1 - slot)
            wait_w(slot)

            def block(i, r):
                gate, up = dot(hs[r, :], pair(wb.at[slot], 0)), dot(hs[r, :], pair(wb.at[slot], 1))
                us[j, r, :] = (jax.nn.gelu(gate, approximate=True) * up).astype(jnp.bfloat16)
            blocks(seq, 2 * MB, block)

        fast = 6
        def two(i, carry):
            gu(2 * i, 0)
            gu(2 * i + 1, 1)
            cm.tick(t0 + done + i)
            return carry
        lax.fori_loop(0, fast, two, 0)
        done += fast

        def one(i, carry):
            gu(2 * fast + i, i % 2)
            cm.tick(t0 + done + i)
            return carry
        singles = nf - 1 - 2 * fast
        lax.fori_loop(0, singles, one, 0)
        done += singles
        gu(nf - 1, (nf - 1) % 2, last=True)

        def lhs_u(r):
            return jnp.concatenate([us[j, r, :] for j in range(nf)], axis=-1)

        need = g_d + nsub + lead - 1 - first
        cm.ticks(t0 + done, need - done)
        done = need
        nbatch = ncol // PIECES
        load_d(base, 0, 0)
        for b in range(nbatch):
            wait_d(b % 2)
            count = nsub if b + 1 < nbatch else pl.cdiv(nsub, PIECES)
            steps = (PIECES // 2) * (seq // MB)

            def d_step(i, carry, b=b):
                p, m = i // (seq // MB), i % (seq // MB)
                r = pl.ds(pl.multiple_of(m * MB, MB), MB)
                w = jnp.concatenate([db[b % 2, 2 * p], db[b % 2, 2 * p + 1]], axis=-1)
                ys[2 * b + p, r, :] = dot(lhs_u(r), w)
                return carry

            def d_tick(i, carry, done=done):
                d_step(i, 0)
                cm.tick(t0 + done + i)
                return carry
            lax.fori_loop(0, count, d_tick, 0)
            done += count
            if b + 1 < nbatch:
                load_d(base, b + 1, (b + 1) % 2)
            else:
                load_tail(base, (b + 1) % 2)
            lax.fori_loop(count, steps, d_step, 0)
        wait_tail(nbatch % 2)

        def fin(i, r):
            tail = dot(lhs_u(r), db[nbatch % 2, 0])
            down = jnp.concatenate([ys[p, r, :] for p in range(ncol // 2)] + [tail], axis=-1)
            res = (x1[r, :].astype(jnp.float32) + rms(down, nw[l, pl.ds(3, 1), :])).astype(jnp.bfloat16)
            xs[r, :] = res
            nxt = jnp.minimum(l + 1, layers - 1)
            hs[r, :] = rms(res.astype(jnp.float32), nw[nxt, pl.ds(0, 1), :]).astype(jnp.bfloat16)
        blocks(seq, MB, fin)
        cm.ticks(t0 + done, per - done)
        return carry

    lax.fori_loop(0, layers, layer, 0)
    out = pltpu.make_async_copy(xs, xo_hbm, iosem.at[0])
    out.start()
    pltpu.make_async_copy(ks, ko_hbm, iosem.at[1]).wait()
    pltpu.make_async_copy(vs, vo_hbm, iosem.at[2]).wait()
    out.wait()


def rope_tables(seq_len, head_dim, rope_base, pos_div):
    half_dim = head_dim // 2
    inv_freq = rope_base ** (-2.0 * jnp.arange(half_dim, dtype=jnp.float32) / head_dim)
    positions = jnp.arange(seq_len, dtype=jnp.float32) / pos_div
    angles = positions[:, None] * inv_freq[None, :]
    return jnp.stack([jnp.cos(angles), jnp.sin(angles)])


def units(rows, l, w_q, w_k, w_v, w_o, w_gate, w_up, w_down):
    def cols(w):
        return w.reshape(w.shape[0], -1, LANES).transpose(1, 0, 2)

    def padded(w, n):
        return jnp.pad(w, ((0, -w.shape[0] % n), (0, 0), (0, 0)))

    qkv = jnp.concatenate([cols(w_q[l]), cols(w_k[l]), cols(w_v[l])])
    o = cols(w_o[l])
    o = padded(jnp.pad(o, ((0, 0), (0, rows - o.shape[1]), (0, 0))), PIECES)
    gate, up = cols(w_gate[l]), cols(w_up[l])
    gu = jnp.stack([gate.reshape(-1, 2, rows, LANES), up.reshape(-1, 2, rows, LANES)], axis=1).reshape(-1, rows, LANES)
    down = w_down[l].reshape(-1, rows, w_down.shape[2] // LANES, LANES)
    whole = down.shape[2] // PIECES * PIECES
    batches = down[:, :, :whole].reshape(down.shape[0], rows, -1, PIECES, LANES).transpose(2, 0, 3, 1, 4)
    tail = padded(down[:, :, whole:].transpose(2, 0, 1, 3).reshape(-1, rows, LANES), PIECES)
    flat = jnp.concatenate([qkv, o, gu, batches.reshape(-1, rows, LANES), tail])
    return flat.reshape(-1, PIECES, rows, LANES)


def solution(mesh):
    batch_spec = P(("dp", "fsdp"), None, None)
    cache_spec = P(("dp", "fsdp"), None, None, None)
    weight_spec = P(None, "fsdp", None)
    side, nz = math.isqrt(mesh.shape["dp"]), mesh.shape["fsdp"] // 2

    def per_device(x, w_q, w_k, w_v, w_o, w_gate, w_up, w_down, norm_w, qk_norm_w):
        layers, rows, qw = w_q.shape
        _, seq, dm = x.shape
        hd = qk_norm_w.shape[-1]
        heads, ffn = qw // hd, w_gate.shape[2]
        scale = (dm // heads if hd == 128 else hd) ** -0.5
        stacked = (w_q, w_k, w_v, w_o, w_gate, w_up, w_down)
        share = jnp.concatenate([units(rows, l, *stacked) for l in range(layers)])
        ng = share.shape[0]
        tab = jnp.stack([rope_tables(seq, hd, ROPE_BASES[l], ROPE_DIVS[l]) for l in range(layers)])
        ncol, nf = dm // LANES, ffn // (2 * LANES)
        cfg = (side, nz, ng, layers, heads, hd, nf, w_down.shape[1] // rows, scale)
        nsem = 2 * (nz // 2) + 4
        bf, f32 = jnp.bfloat16, jnp.float32
        any_spec, vmem = pl.BlockSpec(memory_space=pl.ANY), pl.BlockSpec(memory_space=pltpu.VMEM)
        out = pl.pallas_call(
            functools.partial(kernel, cfg),
            out_shape=(jax.ShapeDtypeStruct((seq, dm), bf), jax.ShapeDtypeStruct((seq, hd), bf),
                       jax.ShapeDtypeStruct((seq, hd), bf),
                       jax.ShapeDtypeStruct((ng, PIECES, nz, 2 * rows, LANES), bf)),
            in_specs=[any_spec, vmem, vmem, vmem, any_spec],
            out_specs=(any_spec,) * 4,
            scratch_shapes=[
                pltpu.VMEM((seq, dm), bf), pltpu.VMEM((seq, dm), bf), pltpu.VMEM((seq, dm), bf),
                pltpu.VMEM((heads, seq, hd), bf), pltpu.VMEM((seq, hd), bf), pltpu.VMEM((seq, hd), bf),
                pltpu.VMEM((heads, seq, hd), bf),
                pltpu.VMEM((ncol, w_o.shape[1] * 2 * nz, LANES), bf),
                pltpu.VMEM((nf, seq, 2 * LANES), bf),
                pltpu.VMEM((ncol // 2, seq, 2 * LANES), f32),
                pltpu.VMEM((2, PIECES, dm, LANES), bf),
                pltpu.VMEM((2, PIECES, ffn, LANES), bf),
                pltpu.SemaphoreType.DMA((nsem, SLOTS)), pltpu.SemaphoreType.DMA((nsem, SLOTS)),
                pltpu.SemaphoreType.DMA((SLOTS,)), pltpu.SemaphoreType.DMA((2,)), pltpu.SemaphoreType.DMA((1,)),
                pltpu.SemaphoreType.DMA((2,)), pltpu.SemaphoreType.DMA((3,)),
            ],
            compiler_params=pltpu.CompilerParams(
                collective_id=0, has_side_effects=True, vmem_limit_bytes=63 * 1024 * 1024),
        )(x.reshape(seq, dm), norm_w, qk_norm_w, tab, share)
        return out[0][None], out[1][None, :, None], out[2][None, :, None]

    in_specs = (batch_spec,) + (weight_spec,) * 7 + (P(), P())
    return jax.shard_map(per_device, mesh=mesh, in_specs=in_specs, out_specs=(batch_spec, cache_spec, cache_spec), check_vma=False)
```

time: 733 us -> 396 us (0.54); the launches traced: 725 us -> 396 us
  Pallas kernels: 0 us -> 342 us
  waiting for transfers between devices: 328 us -> 0 us
  matrix products: 209 us -> 0 us
  blocking collectives: 80.1 us -> 0 us
  other arithmetic: 43.6 us -> 12.5 us
  between operations: 15.2 us -> 0.95 us
    pallas_call x0 -> x1, Pallas kernels: none -> 342 us  [per_device(): pl.pallas_call(functools.partial(kernel, cfg), out_shape=(jax.ShapeDtypeS...]
    all_gather x10 -> x0, waiting for transfers between devices: 325 us -> none  [gather_layer(): lax.all_gather(w_all[layer_idx], 'fsdp', axis=0, tiled=True)]
    dot_general x22 -> x0, matrix products: 209 us -> none  [the longest x2 58.9 us: decoder_layer(): jnp.einsum('nsd,df->nsf', normed_ffn, w_up, preferred_element_type=jnp.fl...]
    all_gather x4 -> x0, blocking collectives: 80.1 us -> none  [gather_layer(): lax.all_gather(w_all[layer_idx], 'fsdp', axis=0, tiled=True)]
    reduce_sum x10 -> x0, other arithmetic: 20.5 us -> none  [the longest x6 11.2 us: rms_norm(): mean_sq = jnp.mean(values * values, axis=-1, keepdims=True)]
    reshape x2, local copies, waits for them, and re-layouts: 10.8 us -> 1.15 us  [units(): down[:, :, :whole].reshape(down.shape[0], rows, -1, PIECES, LANES)]
    another operation x2 -> x14, local copies, waits for them, and re-layouts: 3.72 us -> 11.4 us  [the longest x10 4.95 us: cols(): return w.reshape(w.shape[0], -1, LANES).transpose(1, 0, 2)]
  transfers between devices with their start and end apart: 10 -> 0, of which waited for: 7 -> 0; matrix products, arithmetic and copies ran while one was open for 37% -> 0% of each run, Pallas kernels for 0% -> 0%
where the time goes in v1:
time: 396 us
  Pallas kernels  342 us (86%)
  local copies, waits for them, and re-layouts  40 us (10%)
  other arithmetic  12.5 us (3%)
    pallas_call x1, Pallas kernels, per_device(): pl.pallas_call(functools.partial(kernel, cfg), out_shape=(jax.ShapeDtypeS...  342 us
    unnamed x42, local copies, waits for them, and re-layouts  13.7 us

profile of v1, /device:TPU:22, one launch (start us, length us, event | category | flops | bytes accessed | tf_op | source)
XLA Modules:
  0.0 395.6 jit_solution(12323388725066388225)
XLA Ops:
  0.7 0.8 fusion.9
  1.5 0.6 reshape_squeeze.50
  2.1 0.8 fusion.8
  2.9 0.6 reshape_squeeze.51
  3.5 1.0 slice_bitcast_fusion.1
  4.6 1.0 fusion.7
  5.9 0.7 copy.74
  6.6 1.9 multiply_cosine_fusion
  8.5 1.9 fusion.1
  10.4 0.1 maximum_bitcast_fusion
  10.6 1.5 pad_maximum_fusion.1.tab
  12.0 0.7 copy-done.2
  12.7 0.1 fusion.5
  12.8 0.5 reshape_squeeze.46
  13.4 0.1 copy.53
  13.5 0.5 reshape_squeeze.53
  14.1 1.1 copy.61
  15.2 2.6 fusion.6
  17.8 0.5 reshape_squeeze.47
  18.3 0.1 copy.54
  18.4 0.2 pad_maximum_fusion.2
  18.6 0.2 copy.55
  18.8 1.9 reshape_squeeze.54
  20.7 0.1 copy.62
  20.8 1.5 pad_maximum_fusion.3
  22.4 1.5 copy.63
  23.8 1.1 fusion.4
  24.9 3.3 reshape_squeeze.48
  28.2 1.3 slice.73
  29.5 1.2 slice.72
  30.8 0.7 copy.86
  31.4 1.0 copy.56
  32.5 1.5 reshape_squeeze.55
  33.9 1.4 slice.75
  35.4 1.2 slice.74
  36.9 0.3 constant_dynamic-update-slice_fusion.3
  37.4 0.7 copy_dynamic-update-slice_fusion.1
  38.1 0.6 copy_dynamic-update-slice_fusion.5
  38.7 0.6 copy_dynamic-update-slice_fusion.4
  39.3 0.7 pad_dynamic-update-slice_fusion.1
  40.0 1.5 constant_dynamic-update-slice_fusion.1
  41.5 1.0 constant_dynamic-update-slice_fusion
  42.5 0.7 pad_dynamic-update-slice_fusion.3
  43.1 5.4 %pad_maximum_fusion.s_hbm = bf16[94,4,72,128]{3,2,1,0:T(8,128)(2,1)} fusion(bf16[47,4,72,128]{3,2,1,0:T(8,128)(2,1)S(1)} %bitcast.62, bf16[47,4,72,128]{3,2,1,0:T(8,128)(2,1)} %bitcast.15), kind=kLoop, calls=%fused_computation | loop fusion | flops 3465216 | bytes 13860864 | tf_op jit(solution)/shard_map/concatenate | solution.py:409
  48.5 342.1 %shard_map.121 = (bf16[1024,1152]{1,0:T(8,128)(2,1)}, bf16[1024,256]{1,0:T(8,128)(2,1)}, bf16[1024,256]{1,0:T(8,128)(2,1)}, bf16[94,4,8,144,128]{4,3,2,1,0:T(8,128)(2,1)}) custom-call(bf16[1024,1152]{1,0:T(8,128)(2,1)} %bitcast.68, f32[2,4,1152]{2,1,0:T(4,128)} %nw.1, f32[2,2,256]{2,1,0:T(2,128)} %qkn.1, f32[2,2,1024,128]{3,2,1,0:T(8,128)} %pad_maximum_fusion.1.tab, ...), custom_call_target="tpu_custom_call" | custom-call | tf_op jit(solution)/shard_map/pallas_call | solution.py:417
  390.6 3.3 copy.102
  394.0 0.8 copy.103
  394.8 0.8 copy.104
  (37 shorter events, 0.8 us)
Async XLA Ops:
  10.4 2.3 copy-start.2
  20.8 3.0 copy-start.3
  32.5 4.3 %copy-start.8 = (bf16[72,2,128]{2,1,0:T(2,128)(2,1)S(1)}, bf16[72,2,128]{2,1,0:T(2,128)(2,1)}, u32[]{:S(2)}) copy-start(bf16[72,2,128]{2,1,0:T(2,128)(2,1)} %reshape_squeeze.50) | copy-start | bytes 110596
  33.9 2.9 copy-start.9
  33.9 2.9 copy-start.4
  33.9 3.0 copy-start
  37.2 4.3 %copy-start.1 = (bf16[6,72,2,4,128]{4,1,3,0,2:T(8,128)(2,1)S(1)}, bf16[6,72,2,4,128]{4,1,3,0,2:T(8,128)(2,1)}, u32[]{:S(2)}) copy-start(bf16[6,72,2,4,128]{4,1,3,0,2:T(8,128)(2,1)} %copy.56) | copy-start | bytes 2654212
  37.4 5.1 %copy-start.7 = (bf16[6,72,1,128]{3,1,2,0:T(8,128)(2,1)S(1)}, bf16[6,72,1,128]{3,1,2,0:T(8,128)(2,1)}, u32[]{:S(2)}) copy-start(bf16[6,72,1,128]{3,1,2,0:T(8,128)(2,1)} %copy.86) | copy-start | bytes 331780
  390.6 3.4 copy-start.6
  390.6 4.1 %copy-start.5 = (bf16[1024,256]{1,0:T(8,128)(2,1)S(1)}, bf16[1024,256]{1,0:T(8,128)(2,1)}, u32[]{:S(2)}) copy-start(bf16[1024,256]{1,0:T(8,128)(2,1)} %get-tuple-element.8) | copy-start | bytes 1572868

commit v2 on v1

v2 whole, which is shorter than its diff:
```python
import functools
import math

import jax
import jax.numpy as jnp
import numpy as np
from jax import lax
from jax.experimental import pallas as pl
from jax.experimental.pallas import tpu as pltpu
from jax.sharding import PartitionSpec as P

WINDOW = 1024
NORM_EPS = 1e-6
ROPE_BASES = (10000.0, 1000000.0)
ROPE_DIVS = (1.0, 8.0)
MESH = pl.DeviceIdType.MESH
LANES = 128
DELTA = 2
SLOTS = 8
NW = 3
AHEAD = 6
PIECES = 4


class Plan:
    def __init__(self, weights):
        w_q, w_k, _, w_o, w_gate, _, w_down = weights
        self.rows, self.ncol = w_q.shape[1], w_o.shape[2] // LANES
        self.nsub = w_down.shape[1] // self.rows
        self.kv = w_q.shape[2] // (PIECES * LANES)
        self.o = self.kv + 1
        self.odd = self.o + self.ncol // PIECES
        self.ffn = self.odd + 2
        self.nf = w_gate.shape[2] // (2 * LANES)
        self.down = self.ffn + self.nf
        self.per = self.down + self.ncol // PIECES * self.nsub
        self.halves = self.per - self.nsub


class Comm:
    def __init__(self, side, nz, layers, weights, g_ref, ssem, rsem, lsem):
        self.plan = Plan(weights)
        self.ng, self.nz, self.w, self.g = layers * self.plan.per, nz, weights, g_ref
        self.ssem, self.rsem, self.lsem = ssem, rsem, lsem
        d, f = lax.axis_index("dp"), lax.axis_index("fsdp")
        self.z, self.c = f // 2, f % 2
        xi, yi = d // side, d % side
        a, b = xi % 2, yi % 2
        self.h = (a + b) % 2
        self.up = {"dp": d, "fsdp": ((self.z + 1) % nz) * 2 + self.c}
        self.down = {"dp": d, "fsdp": ((self.z + nz - 1) % nz) * 2 + self.c}
        self.sib = {"dp": d, "fsdp": self.z * 2 + 1 - self.c}
        self.over_x = {"dp": (xi + 1 - 2 * a) * side + yi, "fsdp": f}
        self.over_y = {"dp": xi * side + yi + 1 - 2 * b, "fsdp": f}
        self.hops = nz // 2
        self.stages = self.hops + 2

    def barrier(self):
        bar = pltpu.get_barrier_semaphore()
        peers = (self.up, self.down, self.sib, self.over_x, self.over_y)
        for peer in peers:
            pl.semaphore_signal(bar, inc=1, device_id=peer, device_id_type=MESH)
        pl.semaphore_wait(bar, len(peers))

    def copies(self, k, g, slot):
        rows, nz, n = self.plan.rows, self.nz, 2 * self.hops
        mine = pl.ds(pl.multiple_of(self.c * rows, 8), rows)

        def remote(i, src, dst, peer):
            return pltpu.make_async_remote_copy(
                src_ref=src, dst_ref=dst, send_sem=self.ssem.at[i, slot], recv_sem=self.rsem.at[i, slot],
                device_id=peer, device_id_type=MESH)

        if k < self.hops:
            half = k == self.hops - 1
            pu = pl.ds(2 * self.h, 1 if half else 2)
            pd = pl.ds(2 * self.h + 1, 1) if half else pu
            su, sd = self.g.at[g, pu, (nz - k) % nz, mine], self.g.at[g, pd, k, mine]
            return [remote(2 * k, su, self.g.at[g, pu, nz - 1 - k, mine], self.up),
                    remote(2 * k + 1, sd, self.g.at[g, pd, k + 1, mine], self.down)]
        rest = pl.ds(1, nz - 1)
        if k == self.hops:
            p = 2 * self.h
            px, py = self.g.at[g, p, rest, mine], self.g.at[g, p + 1, rest, mine]
            return [remote(n, px, px, self.over_x), remote(n + 1, py, py, self.over_y)]
        both = self.g.at[g, :, :, mine]
        return [remote(n + 2, both, both, self.sib)]

    def fetch(self, g):
        pn, rows, slot = self.plan, self.plan.rows, g % SLOTS
        w_q, w_k, w_v, w_o, w_gate, w_up, w_down = self.w
        l = g // pn.per
        i = g - l * pn.per
        every = pl.ds(0, rows)

        def cols(first, n=1):
            return pl.ds(pl.multiple_of(first * LANES, LANES), n * LANES)

        def piece(p, src):
            dst = self.g.at[g, p, 0, pl.ds(pl.multiple_of(self.c * rows, 8), src.shape[0])]
            pltpu.make_async_copy(src, dst, self.lsem.at[p, slot]).start()

        def case(low, high, srcs):
            @pl.when((i >= low) & (i < high))
            def _():
                for p, src in enumerate(srcs()):
                    piece(p, src)

        four = range(PIECES)
        last = pn.ncol - 1
        case(0, pn.kv, lambda: [w_q.at[l, :, cols(PIECES * i + p)] for p in four])
        case(pn.kv, pn.o, lambda: [w.at[l, :, cols(p)] for w in (w_k, w_v) for p in range(2)])
        case(pn.o, pn.odd, lambda: [w_o.at[l, :, cols(PIECES * (i - pn.o) + p)] for p in four])

        def down(r, col):
            return w_down.at[l, pl.ds(pl.multiple_of(r * rows, 8), rows), cols(col)]
        case(pn.odd, pn.odd + 1, lambda: [w_o.at[l, :, cols(last)]] + [down(p, last) for p in range(3)])
        case(pn.odd + 1, pn.ffn, lambda: [down(3 + p, last) for p in range(pn.nsub - 3)])
        case(pn.ffn, pn.down, lambda: [w.at[l, :, cols(2 * (i - pn.ffn) + p)] for w in (w_gate, w_up) for p in range(2)])
        m = i - pn.down
        case(pn.down, pn.halves, lambda: [down(m % pn.nsub, PIECES * (m // pn.nsub) + p) for p in four])
        e = i - pn.halves
        n, col = pn.nsub // 2, last - PIECES
        case(pn.halves, pn.per, lambda: [down(2 * (e % n) + p // 2, col + 2 * (e // n) + p % 2) for p in four])

    def fetched(self, g):
        pn, slot = self.plan, g % SLOTS
        i = g % pn.per
        short = self.w[3].shape[1]

        def case(cond, sizes):
            @pl.when(cond)
            def _():
                for p, n in enumerate(sizes):
                    part = self.g.at[g, p, 0, pl.ds(0, n)]
                    pltpu.make_async_copy(part, part, self.lsem.at[p, slot]).wait()

        full = pn.rows
        case((i < pn.o) | (i >= pn.ffn), [full] * PIECES)
        case((i >= pn.o) & (i < pn.odd), [short] * PIECES)
        case(i == pn.odd, [short] + [full] * 3)
        case(i == pn.odd + 1, [full] * (pn.nsub - 3))

    def tick(self, t):
        slot, old = t % SLOTS, (t + SLOTS - DELTA) % SLOTS

        @pl.when(t < self.ng)
        def _():
            self.fetched(t)
            for cp in self.copies(0, t, slot):
                cp.start()

        @pl.when(t + AHEAD < self.ng)
        def _():
            self.fetch(t + AHEAD)

        for k in range(1, self.stages + 1):
            g = t - DELTA * k

            @pl.when((g >= 0) & (g < self.ng))
            def _(k=k, g=g):
                for cp in self.copies(k - 1, g, old):
                    cp.wait()
                if k < self.stages:
                    for cp in self.copies(k, g, slot):
                        cp.start()

    def ticks(self, first, count):
        def body(i, carry):
            self.tick(first + i)
            return carry
        lax.fori_loop(0, count, body, 0)


def rms(values, gain):
    mean_sq = jnp.mean(values * values, axis=-1, keepdims=True)
    return values * lax.rsqrt(mean_sq + NORM_EPS) * (1.0 + gain)


def rope(values, cos_t, sin_t):
    half = values.shape[-1] // 2
    lo, hi = values[:, :half], values[:, half:]
    return jnp.concatenate([lo * cos_t - hi * sin_t, hi * cos_t + lo * sin_t], axis=-1)


def dot(a, b):
    return jnp.dot(a, b, preferred_element_type=jnp.float32)


def kernel(cfg, x_hbm, nw, qkn, *refs):
    layers = cfg[2]
    tabs, weights, refs = refs[:2 * layers], refs[2 * layers:2 * layers + 7], refs[2 * layers + 7:]
    (xo_hbm, ko_hbm, vo_hbm, g_hbm, xs, hs, x1, qs, ks, vs, at, ob, us, ys, yt, wb, db, dt, tab,
     ssem, rsem, lsem, wsem, osem, dsem, iosem) = refs
    side, nz, layers, scale = cfg
    seq, dm = xs.shape
    heads = qs.shape[0]
    cm = Comm(side, nz, layers, weights, g_hbm, ssem, rsem, lsem)
    pn = cm.plan
    rows, nsub, ncol, nf, per = pn.rows, pn.nsub, pn.ncol, pn.nf, pn.per
    rows_o, rows_d = weights[3].shape[1], weights[6].shape[1]
    def fetch_ahead(g, carry):
        cm.fetch(g)
        return carry
    lax.fori_loop(0, AHEAD, fetch_ahead, 0)
    load_x = pltpu.make_async_copy(x_hbm, xs, iosem.at[0])
    load_x.start()
    for i, tab_hbm in enumerate(tabs):
        pltpu.make_async_copy(tab_hbm, tab.at[i // 2, i % 2], iosem.at[3]).start()
    cm.barrier()
    lead = DELTA * cm.stages + 1
    first = lead + pn.kv
    MB = 256

    def place(rel):
        return (cm.z + rel) % nz

    def load_w(g, slot):
        for rel in range(nz):
            dst = wb.at[slot, :, pl.ds(pl.multiple_of(place(rel) * 2 * rows, 16), 2 * rows), :]
            pltpu.make_async_copy(g_hbm.at[g, :, rel], dst, wsem.at[slot]).start()

    def wait_w(slot):
        pltpu.make_async_copy(wb.at[slot], wb.at[slot], wsem.at[slot]).wait()

    def load_o(base):
        for i in range(pl.cdiv(ncol, PIECES)):
            n = min(PIECES, ncol - PIECES * i)
            for rel in range(nz):
                for c in range(2):
                    src = g_hbm.at[base + pn.o + i, pl.ds(0, n), rel, pl.ds(c * rows, rows_o), :]
                    off = pl.multiple_of((place(rel) * 2 + c) * rows_o, 16)
                    dst = ob.at[pl.ds(PIECES * i, n), pl.ds(off, rows_o), :]
                    pltpu.make_async_copy(src, dst, osem.at[0]).start()

    def wait_o():
        pltpu.make_async_copy(ob, ob, osem.at[0]).wait()

    def load_d(base, k, whole):
        def part(pieces, cols, r, sem):
            for rel in range(nz):
                for c in range(2):
                    src = g_hbm.at[base + pn.down + k, pieces, rel, pl.ds(c * rows, rows), :]
                    off = pl.multiple_of((place(rel) * 2 + c) * rows_d + r * rows, 8)
                    pltpu.make_async_copy(src, db.at[cols, pl.ds(off, rows), :], dsem.at[sem]).start()

        if whole:
            part(pl.ds(0, PIECES), pl.ds(0, PIECES), k, 0)
        else:
            e = k - nsub
            half, n = e // (nsub // 2), e % (nsub // 2)
            for q in range(2):
                part(pl.ds(2 * q, 2), pl.ds(PIECES + 2 * half, 2), 2 * n + q, 1 + half)

    def wait_d(first_col, n, sem):
        part = db.at[pl.ds(first_col, n)]
        pltpu.make_async_copy(part, part, dsem.at[sem]).wait()

    def load_odd(base):
        for r in range(nsub):
            for rel in range(nz):
                for c in range(2):
                    src = g_hbm.at[base + pn.odd + (r + 1) // PIECES, (r + 1) % PIECES, rel, pl.ds(c * rows, rows), :]
                    off = pl.multiple_of((place(rel) * 2 + c) * rows_d + r * rows, 8)
                    pltpu.make_async_copy(src, dt.at[pl.ds(off, rows), :], osem.at[1]).start()

    def wait_odd():
        pltpu.make_async_copy(dt, dt, osem.at[1]).wait()

    def blocks(n, size, body):
        def step(i, carry):
            body(i, pl.ds(pl.multiple_of(i * size, size), size))
            return carry
        lax.fori_loop(0, n // size, step, 0)

    load_x.wait()
    pltpu.make_async_copy(tab, tab, iosem.at[3]).wait()

    def start_up(i, r):
        cm.tick(i)
        hs[r, :] = rms(xs[r, :].astype(jnp.float32), nw[0, pl.ds(0, 1), :]).astype(jnp.bfloat16)
    blocks(seq, MB, start_up)
    begun = seq // MB
    cm.ticks(begun, first - begun)

    def pair(ref, p):
        return jnp.concatenate([ref[2 * p], ref[2 * p + 1]], axis=-1)

    def layer(l, carry):
        base = l * per
        t0 = base + first

        for i in range(pn.kv + 1):
            load_w(base + i, i)

        def head_out(r, acc, which):
            out = rms(acc, qkn[l, pl.ds(which, 1), :])
            return rope(out, tab[l, 0, r, :], tab[l, 1, r, :]).astype(jnp.bfloat16)

        def q_group(i, carry):
            wait_w(i)

            def q_block(j, r):
                for p in range(2):
                    qs[2 * i + p, r, :] = head_out(r, dot(hs[r, :], pair(wb.at[i], p)), 0)
            blocks(seq, MB, q_block)
            cm.tick(t0 + i)
            return carry
        lax.fori_loop(0, pn.kv, q_group, 0)
        wait_w(pn.kv)

        def kv_block(j, r):
            ks[r, :] = head_out(r, dot(hs[r, :], pair(wb.at[pn.kv], 0)), 1)
            vs[r, :] = dot(hs[r, :], pair(wb.at[pn.kv], 1)).astype(jnp.bfloat16)
        blocks(seq, MB, kv_block)
        cm.tick(t0 + pn.kv)
        load_o(base)
        done = pn.kv + 1

        @pl.when(l == layers - 1)
        def _():
            pltpu.make_async_copy(ks, ko_hbm, iosem.at[1]).start()
            pltpu.make_async_copy(vs, vo_hbm, iosem.at[2]).start()

        nb = seq // MB
        for b in range(nb):
            r = pl.ds(b * MB, MB)
            span = (b + 1) * MB
            per_tick = heads if b < nb // 2 else heads // 2

            def one_head(j, b=b, r=r, span=span):
                sc = lax.dot_general(qs[j, r, :], ks[pl.ds(0, span), :], (((1,), (1,)), ((), ())),
                                     preferred_element_type=jnp.float32) * scale
                diff = (b * MB + lax.broadcasted_iota(jnp.int32, sc.shape, 0)
                        - lax.broadcasted_iota(jnp.int32, sc.shape, 1))
                allowed = diff >= 0
                if span > WINDOW:
                    allowed = allowed & ((diff < WINDOW) | (l > 0))
                sc = jnp.where(allowed, sc, -1e30)
                e = jnp.exp(sc - jnp.max(sc, axis=-1, keepdims=True))
                probs = (e * (1.0 / jnp.sum(e, axis=-1, keepdims=True))).astype(jnp.bfloat16)
                at[j, r, :] = dot(probs, vs[pl.ds(0, span), :]).astype(jnp.bfloat16)

            def some_heads(i, carry, per_tick=per_tick, done=done, one_head=one_head):
                def body(j, carry):
                    one_head(i * per_tick + j)
                    return carry
                lax.fori_loop(0, per_tick, body, 0)
                cm.tick(t0 + done + i)
                return carry
            lax.fori_loop(0, heads // per_tick, some_heads, 0)
            done += heads // per_tick

        for j in range(2):
            load_w(base + pn.ffn + j, j)
        load_odd(base)
        wait_o()

        def o_block(i, r):
            lhs = jnp.concatenate([at[j, r, :] for j in range(heads)], axis=-1)
            parts = [dot(lhs, pair(ob, p)) for p in range(ncol // 2)]
            if ncol % 2:
                parts.append(dot(lhs, ob[ncol - 1]))
            proj = jnp.concatenate(parts, axis=-1)
            res = (xs[r, :].astype(jnp.float32) + rms(proj, nw[l, pl.ds(1, 1), :])).astype(jnp.bfloat16)
            x1[r, :] = res
            hs[r, :] = rms(res.astype(jnp.float32), nw[l, pl.ds(2, 1), :]).astype(jnp.bfloat16)
        nb = seq // MB

        def o_step(i, carry):
            for m in range(2):
                o_block(0, pl.ds(pl.multiple_of((2 * i + m) * MB, MB), MB))
            cm.tick(t0 + done + i)
            return carry
        lax.fori_loop(0, nb // 2, o_step, 0)
        done += nb // 2

        def gu(j, more=True):
            slot = j % NW
            if more:
                load_w(base + pn.ffn + j + 2, (j + 2) % NW)
            wait_w(slot)

            def block(i, r):
                gate, up = dot(hs[r, :], pair(wb.at[slot], 0)), dot(hs[r, :], pair(wb.at[slot], 1))
                us[j, r, :] = (jax.nn.gelu(gate, approximate=True) * up).astype(jnp.bfloat16)
            blocks(seq, 2 * MB, block)

        fast = first + done - 2 - pn.ffn - lead

        def two(i, carry):
            gu(2 * i)
            gu(2 * i + 1)
            cm.tick(t0 + done + i)
            return carry
        lax.fori_loop(0, fast, two, 0)
        done += fast

        def one(i, carry):
            gu(2 * fast + i)
            cm.tick(t0 + done + i)
            return carry
        singles = nf - 2 - 2 * fast
        lax.fori_loop(0, singles, one, 0)
        done += singles
        def end(i, carry):
            gu(nf - 2 + i, more=False)
            cm.tick(t0 + done + i)
            return carry
        lax.fori_loop(0, 2, end, 0)
        done += 2

        def lhs_u(r):
            return jnp.concatenate([us[j, r, :] for j in range(nf)], axis=-1)

        def d_step(i):
            p, m = i // nb, i % nb
            r = pl.ds(pl.multiple_of(m * MB, MB), MB)
            ys[p, r, :] = dot(lhs_u(r), jnp.concatenate([db[2 * p], db[2 * p + 1]], axis=-1))

        def odd(i):
            r = pl.ds(pl.multiple_of(i * MB, MB), MB)
            yt[r, :] = dot(lhs_u(r), dt[...])

        wait_odd()
        ready = first + done - lead - pn.down + 1
        def load_whole(k, carry):
            load_d(base, k, True)
            return carry
        lax.fori_loop(0, ready, load_whole, 0)

        def odd_step(i, carry):
            odd(i)
            cm.tick(t0 + done + i)
            load_d(base, ready + i, True)
            return carry
        lax.fori_loop(0, nsub - ready, odd_step, 0)
        done += nsub - ready
        for i in range(nsub - ready, nb):
            odd(i)
        wait_d(0, PIECES, 0)

        def d_pair(i, carry):
            @pl.when(i == nb)
            def _():
                wait_d(PIECES, 2, 1)
            d_step(2 * i)
            d_step(2 * i + 1)
            cm.tick(t0 + done + i)
            load_d(base, nsub + i, False)
            return carry
        lax.fori_loop(0, nsub, d_pair, 0)
        done += nsub
        wait_d(PIECES + 2, 2, 2)

        def fin(i, r):
            parts = [ys[p, r, :] for p in range(ncol // 2 - 1)]
            parts += [dot(lhs_u(r), pair(db, ncol // 2 - 1)), yt[r, :]]
            res = (x1[r, :].astype(jnp.float32) + rms(jnp.concatenate(parts, axis=-1), nw[l, pl.ds(3, 1), :])).astype(jnp.bfloat16)
            xs[r, :] = res
            nxt = jnp.minimum(l + 1, layers - 1)
            hs[r, :] = rms(res.astype(jnp.float32), nw[nxt, pl.ds(0, 1), :]).astype(jnp.bfloat16)
        left = per - done

        def fin_tick(i, carry):
            fin(i, pl.ds(pl.multiple_of(i * MB, MB), MB))
            cm.tick(t0 + done + i)
            return carry
        lax.fori_loop(0, min(left, nb), fin_tick, 0)
        for i in range(min(left, nb), nb):
            fin(i, pl.ds(i * MB, MB))
        cm.ticks(t0 + done + nb, left - nb)
        return carry

    lax.fori_loop(0, layers, layer, 0)
    out = pltpu.make_async_copy(xs, xo_hbm, iosem.at[0])
    out.start()
    pltpu.make_async_copy(ks, ko_hbm, iosem.at[1]).wait()
    pltpu.make_async_copy(vs, vo_hbm, iosem.at[2]).wait()
    out.wait()


def rope_tables(seq_len, head_dim, rope_base, pos_div):
    half_dim = head_dim // 2
    inv_freq = (rope_base ** (-2.0 * np.arange(half_dim) / head_dim)).astype(np.float32)
    positions = jnp.arange(seq_len, dtype=jnp.float32) / pos_div
    angles = positions[:, None] * jnp.asarray(inv_freq)[None, :]
    return jnp.cos(angles), jnp.sin(angles)


def solution(mesh):
    batch_spec = P(("dp", "fsdp"), None, None)
    cache_spec = P(("dp", "fsdp"), None, None, None)
    weight_spec = P(None, "fsdp", None)
    side, nz = math.isqrt(mesh.shape["dp"]), mesh.shape["fsdp"] // 2

    def per_device(x, w_q, w_k, w_v, w_o, w_gate, w_up, w_down, norm_w, qk_norm_w):
        layers, rows, qw = w_q.shape
        _, seq, dm = x.shape
        hd = qk_norm_w.shape[-1]
        heads, ffn, ncol, nf = qw // hd, w_gate.shape[2], dm // LANES, w_gate.shape[2] // (2 * LANES)
        scale = (dm // heads if hd == 128 else hd) ** -0.5
        weights = (w_q, w_k, w_v, w_o, w_gate, w_up, w_down)
        ng = layers * Plan(weights).per
        tabs = [t for l in range(layers) for t in rope_tables(seq, hd, ROPE_BASES[l], ROPE_DIVS[l])]
        cfg = (side, nz, layers, scale)
        nsem = 2 * (nz // 2) + 3
        bf, f32 = jnp.bfloat16, jnp.float32
        any_spec, vmem = pl.BlockSpec(memory_space=pl.ANY), pl.BlockSpec(memory_space=pltpu.VMEM)
        out = pl.pallas_call(
            functools.partial(kernel, cfg),
            out_shape=(jax.ShapeDtypeStruct((seq, dm), bf), jax.ShapeDtypeStruct((seq, hd), bf),
                       jax.ShapeDtypeStruct((seq, hd), bf),
                       jax.ShapeDtypeStruct((ng, PIECES, nz, 2 * rows, LANES), bf)),
            in_specs=[any_spec, vmem, vmem] + [any_spec] * (len(tabs) + len(weights)),
            out_specs=(any_spec,) * 4,
            scratch_shapes=[
                pltpu.VMEM((seq, dm), bf), pltpu.VMEM((seq, dm), bf), pltpu.VMEM((seq, dm), bf),
                pltpu.VMEM((heads, seq, hd), bf), pltpu.VMEM((seq, hd), bf), pltpu.VMEM((seq, hd), bf),
                pltpu.VMEM((heads, seq, hd), bf),
                pltpu.VMEM((ncol, w_o.shape[1] * 2 * nz, LANES), bf),
                pltpu.VMEM((nf, seq, 2 * LANES), bf),
                pltpu.VMEM((ncol // 2, seq, 2 * LANES), f32),
                pltpu.VMEM((seq, LANES), f32),
                pltpu.VMEM((NW, PIECES, dm, LANES), bf),
                pltpu.VMEM((ncol - 1, ffn, LANES), bf),
                pltpu.VMEM((ffn, LANES), bf),
                pltpu.VMEM((layers, 2, seq, hd // 2), f32),
                pltpu.SemaphoreType.DMA((nsem, SLOTS)), pltpu.SemaphoreType.DMA((nsem, SLOTS)),
                pltpu.SemaphoreType.DMA((PIECES, SLOTS)), pltpu.SemaphoreType.DMA((NW,)), pltpu.SemaphoreType.DMA((2,)),
                pltpu.SemaphoreType.DMA((3,)), pltpu.SemaphoreType.DMA((4,)),
            ],
            compiler_params=pltpu.CompilerParams(
                collective_id=0, has_side_effects=True, vmem_limit_bytes=63 * 1024 * 1024),
        )(x.reshape(seq, dm), norm_w, qk_norm_w, *tabs, *weights)
        return out[0][None], out[1][None, :, None], out[2][None, :, None]

    in_specs = (batch_spec,) + (weight_spec,) * 7 + (P(), P())
    return jax.shard_map(per_device, mesh=mesh, in_specs=in_specs, out_specs=(batch_spec, cache_spec, cache_spec), check_vma=False)
```

time: 396 us -> 333 us (0.84)
  local copies, waits for them, and re-layouts: 40 us -> 4.93 us
  Pallas kernels: 342 us -> 319 us
  other arithmetic: 12.5 us -> 7.19 us
    pallas_call x1, Pallas kernels: 342 us -> 319 us  [per_device(): pl.pallas_call(functools.partial(kernel, cfg), out_shape=(jax.ShapeDtypeS...]
    slice x10 -> x0, local copies, waits for them, and re-layouts: 11.6 us -> none  [the longest x2 2.73 us: units(): gate, up = (cols(w_gate[l]), cols(w_up[l]))]
    another operation x14 -> x0, local copies, waits for them, and re-layouts: 11.4 us -> none  [the longest x10 4.95 us: cols(): return w.reshape(w.shape[0], -1, LANES).transpose(1, 0, 2)]
    unnamed x42 -> x7, local copies, waits for them, and re-layouts: 13.7 us -> 4.93 us
    sin x0 -> x2, other arithmetic: none -> 7.18 us  [rope_tables(): return (jnp.cos(angles), jnp.sin(angles))]
    concatenate x1 -> x0, other arithmetic: 5.38 us -> none  [per_device(): share = jnp.concatenate([units(rows, l, *stacked) for l in range(layers)])]
where the time goes in v2:
time: 333 us; the launch traced here: 332 us
  Pallas kernels  319 us (96%)
  other arithmetic  7.19 us (2%)
  local copies, waits for them, and re-layouts  4.93 us (1%)
    pallas_call x1, Pallas kernels, per_device(): pl.pallas_call(functools.partial(kernel, cfg), out_shape=(jax.ShapeDtypeS...  319 us
    sin x2, other arithmetic, rope_tables(): return (jnp.cos(angles), jnp.sin(angles))  7.18 us

profile of v2, /device:TPU:22, one launch (start us, length us, event | category | flops | bytes accessed | tf_op | source)
XLA Modules:
  0.0 332.3 jit_solution(14938211386306866377)
XLA Ops:
  0.6 3.7 %multiply_sine_fusion = (f32[1024,128]{1,0:T(8,128)}, f32[1024,128]{1,0:T(8,128)}) fusion(f32[128]{0:T(128)} %constant.9.clone, f32[1024]{0:T(1024)S(1)} %iota_multiply_fusion.1), kind=kLoop, calls=%fused_computation | loop fusion | flops 131072 | bytes 1053184 | tf_op jit(solution)/shard_map/sin | solution.py:488
  4.4 3.4 %fusion = (f32[1024,128]{1,0:T(8,128)}, f32[1024,128]{1,0:T(8,128)}) fusion(f32[128]{0:T(128)} %constant.8.clone), kind=kLoop, calls=%fused_computation.3 | loop fusion | flops 131072 | bytes 1049088 | tf_op jit(solution)/shard_map/sin | solution.py:488
  7.8 319.5 %shard_map.139 = (bf16[1024,1152]{1,0:T(8,128)(2,1)}, bf16[1024,256]{1,0:T(8,128)(2,1)}, bf16[1024,256]{1,0:T(8,128)(2,1)}, bf16[92,4,8,144,128]{4,3,2,1,0:T(8,128)(2,1)}) custom-call(bf16[1024,1152]{1,0:T(8,128)(2,1)} %bitcast.5, f32[2,4,1152]{2,1,0:T(4,128)} %nw.1, f32[2,2,256]{2,1,0:T(2,128)} %qkn.1, f32[1024,128]{1,0:T(8,128)} %get-tuple-element.12.refs_0_, ...), custom_call_target="tpu_custom_call" | custom-call | tf_op jit(solution)/shard_map/pallas_call | solution.py:510
  327.3 0.0 copy-start.1
  327.3 0.0 copy-start
  327.3 3.3 %copy.18 = bf16[1,1024,1152]{2,1,0:T(8,128)(2,1)} copy(bf16[1,1024,1152]{2,1,0:T(8,128)(2,1)} %bitcast.4) | data formatting | bytes 4718592
  330.7 0.0 copy-done.1
  330.7 0.8 copy.19
  331.5 0.0 copy-done
  331.5 0.8 copy.20
  (1 shorter events, 0.0 us)
Async XLA Ops:
  327.3 3.4 %copy-start.1 = (bf16[1024,256]{1,0:T(8,128)(2,1)S(1)}, bf16[1024,256]{1,0:T(8,128)(2,1)}, u32[]{:S(2)}) copy-start(bf16[1024,256]{1,0:T(8,128)(2,1)} %get-tuple-element.7) | copy-start | bytes 1572868
  327.3 4.1 %copy-start = (bf16[1024,256]{1,0:T(8,128)(2,1)S(1)}, bf16[1024,256]{1,0:T(8,128)(2,1)}, u32[]{:S(2)}) copy-start(bf16[1024,256]{1,0:T(8,128)(2,1)} %get-tuple-element.8) | copy-start | bytes 1572868
